TPU v7x, 8 devices: a whole 2x2x1 slice. The times are simulated.
8 devices in a mesh: emb: 8 (over z, y, x, core).
Axes of the slice: x: 2, y: 2, z: 1, core: 2. Of those that a mesh axis runs over, the one named last changes fastest.
Arguments:
- x_start: bfloat16 [16384, 768], P('emb')
- d_out: bfloat16 [16384, 768], P('emb')
- token_ids: int32 [2, 16384, 1], P(None, 'emb')
- w_up: bfloat16 [8, 768, 3072], replicated
- w_down: bfloat16 [8, 3072, 768], replicated
- w_gate: bfloat16 [2, 768, 768], replicated
- w_proj: bfloat16 [2, 768, 768], replicated
- tables: bfloat16 [2, 50304, 768], P(None, 'emb')
Outputs:
- output 1: bfloat16 [16384, 768], P('emb')
- output 2: float32 [2, 50304, 768], P(None, 'emb')
All inputs are finite; a program needn't handle non-finite values.
Results may differ from a plain program's by a relative error of at most 0.02.
Values are sent between devices in bfloat16 or wider.
A program may use at most 1 GiB of HBM per device.

v0:
```python
import jax
import jax.numpy as jnp
from jax import lax
from jax.sharding import PartitionSpec as P

EPS = 1e-6


def gelu_fn(pre_act):
    return jax.nn.gelu(pre_act, approximate=True)


def gelu_grad(pre_act, cotangent):
    _, pullback = jax.vjp(gelu_fn, pre_act.astype(jnp.float32))
    return pullback(cotangent)[0]


def norm_fwd(x_res):
    x_f = x_res.astype(jnp.float32)
    inv_rms = lax.rsqrt(jnp.mean(x_f * x_f, axis=-1, keepdims=True) + EPS)
    return (x_f * inv_rms).astype(jnp.bfloat16), inv_rms


def norm_bwd(x_res, inv_rms, d_norm):
    x_f = x_res.astype(jnp.float32)
    mean_dot = jnp.mean(x_f * d_norm, axis=-1, keepdims=True)
    return inv_rms * d_norm - x_f * (inv_rms * inv_rms * inv_rms) * mean_dot


def slot_map(layers):
    return {1: 0, layers - 1: 1}


def stack_forward(x_start, w_up, w_down, w_gate, w_proj, fetch_rows):
    layers = w_up.shape[0]
    slot_of = slot_map(layers)
    saved_acts = []
    x_cur = x_start
    for layer_idx in range(layers):
        normed, inv_rms = norm_fwd(x_cur)
        hidden = jnp.dot(normed, w_up[layer_idx], preferred_element_type=jnp.float32).astype(jnp.bfloat16)
        activated = gelu_fn(hidden.astype(jnp.float32)).astype(jnp.bfloat16)
        mlp_out = jnp.dot(activated, w_down[layer_idx], preferred_element_type=jnp.float32).astype(jnp.bfloat16)
        new_res = x_cur.astype(jnp.float32) + mlp_out.astype(jnp.float32)
        gate_saved = None
        if layer_idx in slot_of:
            which = slot_of[layer_idx]
            emb_rows = fetch_rows(which)
            pre_gate = jnp.dot(normed, w_gate[which], preferred_element_type=jnp.float32).astype(jnp.bfloat16)
            gate_val = gelu_fn(pre_gate.astype(jnp.float32)).astype(jnp.bfloat16)
            mixed_val = (gate_val.astype(jnp.float32) * emb_rows.astype(jnp.float32)).astype(jnp.bfloat16)
            proj_out = jnp.dot(mixed_val, w_proj[which], preferred_element_type=jnp.float32).astype(jnp.bfloat16)
            new_res = new_res + proj_out.astype(jnp.float32)
            gate_saved = (pre_gate, gate_val, emb_rows)
        saved_acts.append((x_cur, inv_rms, hidden, gate_saved))
        x_cur = new_res.astype(jnp.bfloat16)
    return x_cur, saved_acts


def stack_backward(d_out, w_up, w_down, w_gate, w_proj, saved_acts, return_rows):
    layers = w_up.shape[0]
    slot_of = slot_map(layers)
    table_grads = [None, None]
    d_res = d_out.astype(jnp.float32)
    for layer_idx in reversed(range(1, layers)):
        x_prev, inv_rms, hidden, gate_saved = saved_acts[layer_idx]
        d_low = d_res.astype(jnp.bfloat16)
        if gate_saved is not None:
            which = slot_of[layer_idx]
            pre_gate, gate_val, emb_rows = gate_saved
            d_mix = jnp.einsum('td,ed->te', d_low, w_proj[which], preferred_element_type=jnp.float32)
            table_grads[which] = return_rows(which, gate_val.astype(jnp.float32) * d_mix)
        if layer_idx > 1:
            d_act = jnp.einsum('td,fd->tf', d_low, w_down[layer_idx], preferred_element_type=jnp.float32)
            d_hid = gelu_grad(hidden, d_act)
            d_norm = jnp.einsum('tf,df->td', d_hid.astype(jnp.bfloat16), w_up[layer_idx], preferred_element_type=jnp.float32)
            if gate_saved is not None:
                d_gate = gelu_grad(pre_gate, d_mix * emb_rows.astype(jnp.float32))
                d_norm = d_norm + jnp.einsum('te,de->td', d_gate.astype(jnp.bfloat16), w_gate[which], preferred_element_type=jnp.float32)
            d_res = d_res + norm_bwd(x_prev, inv_rms, d_norm)
    return table_grads


def route_plan(flat_ids, rows_dev, n_dev, capacity):
    owner_ids = flat_ids // rows_dev
    sort_order = jnp.argsort(owner_ids, stable=True)
    sorted_owner = owner_ids[sort_order]
    counts = jax.ops.segment_sum(jnp.ones_like(owner_ids), owner_ids, num_segments=n_dev)
    starts = jnp.cumsum(counts) - counts
    sorted_slot = sorted_owner * capacity + jnp.arange(flat_ids.shape[0], dtype=jnp.int32) - starts[sorted_owner]
    return jnp.zeros_like(flat_ids).at[sort_order].set(sorted_slot)


def solution(mesh):
    n_dev = mesh.shape['emb']
    tok_spec = P('emb', None)
    tab_spec = P(None, 'emb', None)

    def local_program(x_start, d_out, token_ids, w_up, w_down, w_gate, w_proj, tables):
        n_tok, n_heads = token_ids.shape[1], token_ids.shape[2]
        rows_dev, row_width = tables.shape[1], tables.shape[2]
        capacity = max(8, (4 * n_tok * n_heads) // n_dev)
        my_base = lax.axis_index('emb') * rows_dev
        pad_ids = (jnp.arange(n_dev * capacity, dtype=jnp.int32) // capacity) * rows_dev
        routes = {}

        def fetch_rows(which):
            flat_ids = token_ids[which].reshape(n_tok * n_heads)
            dest_slot = route_plan(flat_ids, rows_dev, n_dev, capacity)
            send_ids = pad_ids.at[dest_slot].set(flat_ids)
            recv_ids = lax.all_to_all(send_ids, 'emb', 0, 0, tiled=True)
            local_ids = recv_ids - my_base
            served = tables[which][local_ids]
            back_rows = lax.all_to_all(served, 'emb', 0, 0, tiled=True)
            routes[which] = (dest_slot, local_ids)
            return back_rows[dest_slot].reshape(n_tok, n_heads * row_width)

        def return_rows(which, grad_rows):
            dest_slot, local_ids = routes[which]
            send_grad = jnp.zeros((n_dev * capacity, row_width), jnp.float32).at[dest_slot].set(grad_rows.reshape(n_tok * n_heads, row_width))
            recv_grad = lax.all_to_all(send_grad, 'emb', 0, 0, tiled=True)
            return jax.ops.segment_sum(recv_grad, local_ids, num_segments=rows_dev)

        x_end, saved_acts = stack_forward(x_start, w_up, w_down, w_gate, w_proj, fetch_rows)
        table_grads = stack_backward(d_out, w_up, w_down, w_gate, w_proj, saved_acts, return_rows)
        return x_end, jnp.stack(table_grads)

    return jax.shard_map(local_program, mesh=mesh, in_specs=(tok_spec, tok_spec, tab_spec, P(), P(), P(), P(), tab_spec), out_specs=(tok_spec, tab_spec), check_vma=False)
```

profile of v0, /device:TPU:0, one launch (start us, length us, event | category | flops | bytes accessed | tf_op | source)
XLA Modules:
  0.0 1579.3 jit_solution(17190093322626607070)
XLA Ops:
  138.0 42.0 %gather_fusion.1 = bf16[8192,768]{1,0:T(8,128)(2,1)} fusion(bf16[6288,768]{1,0:T(8,128)(2,1)} %get-tuple-element.13, s32[8192]{0:T(1024)S(1)} %broadcast_clamp_fusion.1), kind=kCustom, calls=%fused_computation.1 | custom fusion | bytes 25198592 | tf_op jit(solution)/shard_map/gather | solution.py:113
  192.7 41.3 %fusion.129 = (f32[2048]{0:T(1024)S(1)}, bf16[2048,768]{0,1:T(8,128)(2,1)}) fusion(bf16[8,3072,768]{2,1,0:T(8,128)(2,1)} %param.12, bf16[8,768,3072]{2,1,0:T(8,128)(2,1)} %param.11, bf16[2048,768]{0,1:T(8,128)(2,1)S(1)} %copy.20, f32[2048]{0:T(1024)S(1)} %add_rsqrt_fusion.7), kind=kOutput, calls=%fused_computation.222 | convolution fusion | flops 19413858304 | bytes 18890752 | tf_op jit(solution)/shard_map/dot_general | solution.py:43
  246.4 42.4 %gather_fusion.4 = bf16[8192,768]{1,0:T(8,128)(2,1)} fusion(bf16[6288,768]{1,0:T(8,128)(2,1)} %get-tuple-element.12, s32[8192]{0:T(1024)S(1)} %broadcast_clamp_fusion), kind=kCustom, calls=%fused_computation.4 | custom fusion | bytes 25198592 | tf_op jit(solution)/shard_map/gather | solution.py:113
  288.8 34.2 %all-to-all-done.1 = bf16[8,1024,768]{2,1,0:T(8,128)(2,1)} async-done(((bf16[8,1024,768]{2,1,0:T(8,128)(2,1)}), bf16[8,1024,768]{2,1,0:T(8,128)(2,1)}, u32[]{:S(2)}, u32[]{:S(2)}) %all-to-all-start.1) | async-done | bytes 12582944 | tf_op jit(solution)/shard_map/all_to_all | solution.py:114
  327.4 16.3 %gather_fusion.2 = bf16[2048,768]{1,0:T(8,128)(2,1)} fusion(bf16[8192,768]{1,0:T(8,128)(2,1)} %bitcast.26, s32[2048]{0:T(1024)S(1)} %copy-done.26), kind=kCustom, calls=%fused_computation.2 | custom fusion | bytes 6299648 | tf_op jit(solution)/shard_map/gather | solution.py:116
  350.1 28.8 %fusion.139 = (f32[2048]{0:T(1024)S(1)}, bf16[2048,768]{0,1:T(8,128)(2,1)S(1)}) fusion(bf16[2048,768]{0,1:T(8,128)(2,1)} %convolution_convert_fusion.8, bf16[8,3072,768]{2,1,0:T(8,128)(2,1)} %param.12, bf16[8,768,3072]{2,1,0:T(8,128)(2,1)} %param.11, bf16[2048,768]{0,1:T(8,128)(2,1)} %get-tuple-element.55, f32[2048]{0:T(1024)S(1)} %add_rsqrt_fusion.6), kind=kOutput, calls=%fused_computation.232 | convolution fusion | flops 19417004032 | bytes 22036480 | tf_op jit(solution)/shard_map/dot_general | solution.py:43
  380.5 15.2 convolution_convert_fusion.5
  395.7 17.0 %fusion.147 = (f32[2048]{0:T(1024)S(1)}, bf16[2048,768]{0,1:T(8,128)(2,1)S(1)}) fusion(bf16[8,3072,768]{2,1,0:T(8,128)(2,1)} %param.12, bf16[2048,3072]{1,0:T(8,128)(2,1)} %convolution_convert_fusion.5, bf16[2048,768]{0,1:T(8,128)(2,1)S(1)} %get-tuple-element.57), kind=kOutput, calls=%fused_computation.240 | convolution fusion | flops 9739171840 | bytes 23601152 | tf_op jit(solution)/shard_map/dot_general | solution.py:43
  429.1 17.3 %fusion.154 = (f32[2048]{0:T(1024)S(1)}, bf16[2048,768]{0,1:T(8,128)(2,1)S(1)}) fusion(bf16[8,3072,768]{2,1,0:T(8,128)(2,1)} %param.12, bf16[2048,3072]{1,0:T(8,128)(2,1)} %convolution_convert_fusion.4, bf16[2048,768]{0,1:T(8,128)(2,1)S(1)} %get-tuple-element.59), kind=kOutput, calls=%fused_computation.247 | convolution fusion | flops 9739171840 | bytes 23601152 | tf_op jit(solution)/shard_map/dot_general | solution.py:43
  462.8 17.4 %fusion.161 = (f32[2048]{0:T(1024)S(1)}, bf16[2048,768]{0,1:T(8,128)(2,1)S(1)}) fusion(bf16[8,3072,768]{2,1,0:T(8,128)(2,1)} %param.12, bf16[2048,3072]{1,0:T(8,128)(2,1)} %convolution_convert_fusion.3, bf16[2048,768]{0,1:T(8,128)(2,1)S(1)} %get-tuple-element.61), kind=kOutput, calls=%fused_computation.254 | convolution fusion | flops 9739171840 | bytes 23601152 | tf_op jit(solution)/shard_map/dot_general | solution.py:43
  496.6 17.6 %fusion.168 = (f32[2048]{0:T(1024)S(1)}, bf16[2048,768]{0,1:T(8,128)(2,1)S(1)}) fusion(bf16[8,3072,768]{2,1,0:T(8,128)(2,1)} %param.12, bf16[2048,3072]{1,0:T(8,128)(2,1)} %convolution_convert_fusion.2, bf16[2048,768]{0,1:T(8,128)(2,1)S(1)} %get-tuple-element.63), kind=kOutput, calls=%fused_computation.261 | convolution fusion | flops 9739171840 | bytes 23601152 | tf_op jit(solution)/shard_map/dot_general | solution.py:43
  530.6 17.3 %fusion.175 = (f32[2048]{0:T(1024)S(1)}, bf16[2048,768]{0,1:T(8,128)(2,1)S(1)}) fusion(bf16[8,3072,768]{2,1,0:T(8,128)(2,1)} %param.12, bf16[2048,3072]{1,0:T(8,128)(2,1)} %convolution_convert_fusion.1, bf16[2048,768]{0,1:T(8,128)(2,1)S(1)} %get-tuple-element.65), kind=kOutput, calls=%fused_computation.268 | convolution fusion | flops 9739171840 | bytes 23601152 | tf_op jit(solution)/shard_map/dot_general | solution.py:43
  553.1 15.9 %convolution_convert_fusion = bf16[2048,3072]{1,0:T(8,128)(2,1)} fusion(bf16[8,768,3072]{2,1,0:T(8,128)(2,1)} %param.11, bf16[2048,768]{0,1:T(8,128)(2,1)S(1)} %get-tuple-element.67, f32[2048]{0:T(1024)S(1)} %get-tuple-element.29), kind=kOutput, calls=%fused_computation.180 | convolution fusion | flops 9674686464 | bytes 20455424 | tf_op jit(solution)/shard_map/dot_general | solution.py:41
  569.0 29.8 %fusion.245.clone.5 = bf16[2048,3072]{1,0:T(8,128)(2,1)} fusion(bf16[2048,3072]{1,0:T(8,128)(2,1)} %convolution_convert_fusion, bf16[2048,768]{1,0:T(8,128)(2,1)S(1)} %copy-done.12, bf16[8,3072,768]{2,1,0:T(8,128)(2,1)} %param.12), kind=kOutput, calls=%fused_computation.63.clone.clone.clone.clone.clone.clone.2 | convolution fusion | flops 9795796992 | bytes 33030144 | tf_op jit(solution)/shard_map/td,fd->tf/dot_general | solution.py:74
  598.8 16.2 %gather_fusion.5 = bf16[2048,768]{1,0:T(8,128)(2,1)} fusion(bf16[8192,768]{1,0:T(8,128)(2,1)} %bitcast.62, s32[2048]{0:T(1024)S(1)} %copy-done.27), kind=kCustom, calls=%fused_computation.5 | custom fusion | bytes 6299648 | tf_op jit(solution)/shard_map/gather | solution.py:116
  625.9 16.4 %fusion.182 = (f32[2048]{0:T(1024)S(1)}, f32[2048,768]{0,1:T(8,128)S(1)}) fusion(bf16[2048,768]{0,1:T(8,128)(2,1)} %copy-done.13, f32[2048,768]{0,1:T(8,128)} %fusion.359, bf16[8,768,3072]{2,1,0:T(8,128)(2,1)} %param.11, bf16[2048,3072]{1,0:T(8,128)(2,1)} %fusion.245.clone.5), kind=kOutput, calls=%fused_computation.275 | convolution fusion | flops 9669965824 | bytes 33038336 | tf_op jit(solution)/shard_map/tf,df->td/dot_general | solution.py:76
  642.3 33.7 %fusion.101.clone.5 = bf16[2048,3072]{1,0:T(8,128)(2,1)} fusion(bf16[2048,3072]{1,0:T(8,128)(2,1)} %convolution_convert_fusion.1, bf16[8,3072,768]{2,1,0:T(8,128)(2,1)} %param.12, bf16[2048,768]{0,1:T(8,128)(2,1)S(1)} %copy-done.14, f32[2048,768]{0,1:T(8,128)S(1)} %get-tuple-element.69, bf16[2048,768]{0,1:T(8,128)(2,1)S(1)} %copy-done, ...), kind=kOutput, calls=%fused_computation.66.clone.clone.clone.clone.2 | convolution fusion | flops 9808379904 | bytes 42491904 | tf_op jit(solution)/shard_map/td,fd->tf/dot_general | solution.py:74
  697.3 31.5 %fusion.99.clone.5 = bf16[2048,3072]{1,0:T(8,128)(2,1)} fusion(bf16[2048,3072]{1,0:T(8,128)(2,1)} %convolution_convert_fusion.2, bf16[8,3072,768]{2,1,0:T(8,128)(2,1)} %param.12, f32[2048,768]{0,1:T(8,128)S(1)} %fusion.173), kind=kOutput, calls=%fused_computation.69.clone.clone.clone.clone.2 | convolution fusion | flops 9797369856 | bytes 36175872 | tf_op jit(solution)/shard_map/td,fd->tf/dot_general | solution.py:74
  728.9 15.2 fusion.167
  744.1 32.5 %fusion.97.clone.5 = bf16[2048,3072]{1,0:T(8,128)(2,1)} fusion(bf16[2048,3072]{1,0:T(8,128)(2,1)} %convolution_convert_fusion.3, bf16[8,3072,768]{2,1,0:T(8,128)(2,1)} %param.12, f32[2048,768]{0,1:T(8,128)S(1)} %fusion.173, bf16[2048,768]{0,1:T(8,128)(2,1)} %copy-done.11, f32[2048,768]{0,1:T(8,128)S(1)} %get-tuple-element.73, ...), kind=kOutput, calls=%fused_computation.72.clone.clone.clone.clone.2 | convolution fusion | flops 9806807040 | bytes 45637632 | tf_op jit(solution)/shard_map/td,fd->tf/dot_general | solution.py:74
  776.7 16.8 %fusion.160 = (f32[2048]{0:T(1024)S(1)}, f32[2048,768]{0,1:T(8,128)}) fusion(bf16[2048,768]{0,1:T(8,128)(2,1)} %copy-done.9, bf16[8,768,3072]{2,1,0:T(8,128)(2,1)} %param.11, bf16[2048,3072]{1,0:T(8,128)(2,1)} %fusion.97.clone.5), kind=kOutput, calls=%fused_computation.253 | convolution fusion | flops 9668392960 | bytes 26746880 | tf_op jit(solution)/shard_map/tf,df->td/dot_general | solution.py:76
  800.7 31.8 %fusion.95.clone.5 = bf16[2048,3072]{1,0:T(8,128)(2,1)} fusion(bf16[2048,3072]{1,0:T(8,128)(2,1)} %convolution_convert_fusion.4, bf16[8,3072,768]{2,1,0:T(8,128)(2,1)} %param.12, f32[2048,768]{0,1:T(8,128)S(1)} %fusion.159), kind=kOutput, calls=%fused_computation.75.clone.clone.clone.clone.2 | convolution fusion | flops 9797369856 | bytes 36175872 | tf_op jit(solution)/shard_map/td,fd->tf/dot_general | solution.py:74
  847.6 30.4 %fusion.93.clone.5 = bf16[2048,3072]{1,0:T(8,128)(2,1)} fusion(bf16[2048,3072]{1,0:T(8,128)(2,1)} %convolution_convert_fusion.5, bf16[8,3072,768]{2,1,0:T(8,128)(2,1)} %param.12, f32[2048,768]{0,1:T(8,128)S(1)} %fusion.159, bf16[2048,768]{0,1:T(8,128)(2,1)} %copy-done.6, f32[2048,768]{0,1:T(8,128)S(1)} %get-tuple-element.77, ...), kind=kOutput, calls=%fused_computation.78.clone.clone.clone.clone.2 | convolution fusion | flops 9806807040 | bytes 45637632 | tf_op jit(solution)/shard_map/td,fd->tf/dot_general | solution.py:74
  878.0 17.1 %fusion.146 = (f32[2048]{0:T(1024)S(1)}, f32[2048,768]{0,1:T(8,128)}) fusion(bf16[2048,768]{0,1:T(8,128)(2,1)} %copy-done.4, bf16[8,768,3072]{2,1,0:T(8,128)(2,1)} %param.11, bf16[2048,3072]{1,0:T(8,128)(2,1)} %fusion.93.clone.5), kind=kOutput, calls=%fused_computation.239 | convolution fusion | flops 9668392960 | bytes 26746880 | tf_op jit(solution)/shard_map/tf,df->td/dot_general | solution.py:76
  907.1 20.6 %scatter_custom_fusion.6 = f32[8192,768]{1,0:T(8,128)} fusion(s32[2048]{0:T(1024)} %copy-done.18, f32[]{:T(128)} %constant.75.clone.1, f32[2048,768]{1,0:T(8,128)} %fusion.324, bf16[2048,768]{1,0:T(8,128)(2,1)} %copy-done.3), kind=kCustom, calls=%fused_computation.129 | custom fusion | flops 3145728 | bytes 34603520 | tf_op jit(solution)/shard_map/scatter | solution.py:120
  933.2 22.6 %scatter_custom_fusion.8 = f32[8192,768]{1,0:T(8,128)} fusion(s32[2048]{0:T(1024)} %copy-done.19, f32[]{:T(128)} %constant.75.clone.1, f32[2048,768]{1,0:T(8,128)} %fusion.400, bf16[2048,768]{1,0:T(8,128)(2,1)S(1)} %copy-done.8), kind=kCustom, calls=%fused_computation.127 | custom fusion | flops 18874368 | bytes 34603520 | tf_op jit(solution)/shard_map/scatter | solution.py:120
  955.8 251.3 %all-to-all-done.4 = f32[8,1024,768]{2,1,0:T(8,128)} async-done(((f32[8,1024,768]{2,1,0:T(8,128)}), f32[8,1024,768]{2,1,0:T(8,128)}, u32[]{:S(2)}, u32[]{:S(2)}) %all-to-all-start.4) | async-done | bytes 25165856 | tf_op jit(solution)/shard_map/all_to_all | solution.py:121
  1220.1 18.3 %fusion.178 = bf16[2048,768]{0,1:T(8,128)(2,1)S(1)} fusion(bf16[2048,768]{0,1:T(8,128)(2,1)} %copy-done.13, bf16[2048,768]{0,1:T(8,128)(2,1)} %convolution_convert_fusion.6, bf16[8,3072,768]{2,1,0:T(8,128)(2,1)} %param.12, bf16[2048,3072]{1,0:T(8,128)(2,1)} %convolution_convert_fusion), kind=kOutput, calls=%fused_computation.271 | convolution fusion | flops 9737601024 | bytes 26738688 | tf_op jit(solution)/shard_map/dot_general | solution.py:43
  1241.5 64.9 %scatter_custom_fusion.7 = f32[6288,768]{1,0:T(8,128)} fusion(s32[8192]{0:T(1024)} %bitcast.321, f32[8192,768]{1,0:T(8,128)} %bitcast.66, f32[]{:T(128)} %constant.75.clone.1), kind=kCustom, calls=%fused_computation.192 | custom fusion | flops 6291456 | bytes 19317248 | tf_op jit(solution)/shard_map/scatter-add | solution.py:122
  1306.3 180.2 %all-to-all-done.5 = f32[8,1024,768]{2,1,0:T(8,128)} async-done(((f32[8,1024,768]{2,1,0:T(8,128)}), f32[8,1024,768]{2,1,0:T(8,128)}, u32[]{:S(2)}, u32[]{:S(2)}) %all-to-all-start.5) | async-done | bytes 25165856 | tf_op jit(solution)/shard_map/all_to_all | solution.py:121
  1486.5 64.9 %scatter_custom_fusion.9 = f32[6288,768]{1,0:T(8,128)} fusion(s32[8192]{0:T(1024)} %bitcast.323, f32[8192,768]{1,0:T(8,128)} %bitcast.70, f32[]{:T(128)} %constant.75.clone.1), kind=kCustom, calls=%fused_computation.190 | custom fusion | flops 6291456 | bytes 19317248 | tf_op jit(solution)/shard_map/scatter-add | solution.py:122
  1551.4 27.5 %pad_maximum_fusion = f32[2,6288,768]{2,1,0:T(8,128)} fusion(f32[1,6288,768]{2,1,0:T(8,128)} %bitcast.317, f32[1,6288,768]{2,1,0:T(8,128)} %bitcast.316), kind=kLoop, calls=%fused_computation.54 | loop fusion | flops 9658368 | bytes 77266944 | tf_op jit(solution)/shard_map/stack | solution.py:126
  (162 shorter events, 333.2 us)
Async XLA Ops:
  48.9 10.8 copy-start.18
  59.6 74.7 %all-to-all-start = ((s32[8,1024,1]{1,2,0:T(1,128)}), s32[8,1024,1]{1,2,0:T(1,128)S(1)}, u32[]{:S(2)}, u32[]{:S(2)}) async-start(s32[8,1024,1]{1,2,0:T(1,128)} %bitcast.22), calls=%async_computation | async-start | bytes 65536 | tf_op jit(solution)/shard_map/all_to_all | solution.py:111
  134.4 45.6 %all-to-all-start.2 = ((s32[8,1024,1]{1,2,0:T(1,128)}), s32[8,1024,1]{1,2,0:T(1,128)S(1)}, u32[]{:S(2)}, u32[]{:S(2)}) async-start(s32[8,1024,1]{1,2,0:T(1,128)} %bitcast.58), calls=%async_computation.2 | async-start | bytes 65536 | tf_op jit(solution)/shard_map/all_to_all | solution.py:111
  180.0 143.1 %all-to-all-start.1 = ((bf16[8,1024,768]{2,1,0:T(8,128)(2,1)}), bf16[8,1024,768]{2,1,0:T(8,128)(2,1)}, u32[]{:S(2)}, u32[]{:S(2)}) async-start(bf16[8,1024,768]{2,1,0:T(8,128)(2,1)} %bitcast.319), calls=%async_computation.1 | async-start | bytes 25165824 | tf_op jit(solution)/shard_map/all_to_all | solution.py:114
  245.7 97.9 %copy-start.3 = (bf16[2048,768]{1,0:T(8,128)(2,1)}, bf16[2048,768]{1,0:T(8,128)(2,1)S(1)}, u32[]{:S(2)}) copy-start(bf16[2048,768]{1,0:T(8,128)(2,1)S(1)} %fusion.138) | copy-start | bytes 9437188
  323.1 275.8 %all-to-all-start.3 = ((bf16[8,1024,768]{2,1,0:T(8,128)(2,1)}), bf16[8,1024,768]{2,1,0:T(8,128)(2,1)}, u32[]{:S(2)}, u32[]{:S(2)}) async-start(bf16[8,1024,768]{2,1,0:T(8,128)(2,1)} %bitcast.318), calls=%async_computation.3 | async-start | bytes 25165824 | tf_op jit(solution)/shard_map/all_to_all | solution.py:114
  378.9 16.8 %copy-start.4 = (bf16[2048,768]{0,1:T(8,128)(2,1)}, bf16[2048,768]{0,1:T(8,128)(2,1)S(1)}, u32[]{:S(2)}) copy-start(bf16[2048,768]{0,1:T(8,128)(2,1)S(1)} %get-tuple-element.57) | copy-start | bytes 9437188
  412.7 16.4 %copy-start.6 = (bf16[2048,768]{0,1:T(8,128)(2,1)}, bf16[2048,768]{0,1:T(8,128)(2,1)S(1)}, u32[]{:S(2)}) copy-start(bf16[2048,768]{0,1:T(8,128)(2,1)S(1)} %get-tuple-element.59) | copy-start | bytes 9437188
  446.5 16.3 %copy-start.9 = (bf16[2048,768]{0,1:T(8,128)(2,1)}, bf16[2048,768]{0,1:T(8,128)(2,1)S(1)}, u32[]{:S(2)}) copy-start(bf16[2048,768]{0,1:T(8,128)(2,1)S(1)} %get-tuple-element.61) | copy-start | bytes 9437188
  480.2 16.4 %copy-start.11 = (bf16[2048,768]{0,1:T(8,128)(2,1)}, bf16[2048,768]{0,1:T(8,128)(2,1)S(1)}, u32[]{:S(2)}) copy-start(bf16[2048,768]{0,1:T(8,128)(2,1)S(1)} %get-tuple-element.63) | copy-start | bytes 9437188
  514.2 16.4 %copy-start.15 = (bf16[2048,768]{0,1:T(8,128)(2,1)}, bf16[2048,768]{0,1:T(8,128)(2,1)S(1)}, u32[]{:S(2)}) copy-start(bf16[2048,768]{0,1:T(8,128)(2,1)S(1)} %get-tuple-element.65) | copy-start | bytes 9437188
  553.1 62.0 %copy-start.7 = (bf16[2048,768]{1,0:T(8,128)(2,1)}, bf16[2048,768]{1,0:T(8,128)(2,1)S(1)}, u32[]{:S(2)}) copy-start(bf16[2048,768]{1,0:T(8,128)(2,1)S(1)} %convolution_convert_fusion.7) | copy-start | bytes 9437188
  553.1 15.9 %copy-start.12 = (bf16[2048,768]{1,0:T(8,128)(2,1)S(1)}, bf16[2048,768]{1,0:T(8,128)(2,1)}, u32[]{:S(2)}) copy-start(bf16[2048,768]{1,0:T(8,128)(2,1)} %param.9) | copy-start | bytes 9437188
  569.0 29.8 %copy-start.27 = (s32[2048]{0:T(1024)S(1)}, s32[2048]{0:T(1024)}, u32[]{:S(2)}) copy-start(s32[2048]{0:T(1024)} %get-tuple-element.30) | copy-start | bytes 24580
  625.9 16.4 %copy-start = (bf16[2048,768]{0,1:T(8,128)(2,1)S(1)}, bf16[2048,768]{0,1:T(8,128)(2,1)}, u32[]{:S(2)}) copy-start(bf16[2048,768]{0,1:T(8,128)(2,1)} %copy.25) | copy-start | bytes 9437188
  625.9 16.4 %copy-start.14 = (bf16[2048,768]{0,1:T(8,128)(2,1)S(1)}, bf16[2048,768]{0,1:T(8,128)(2,1)}, u32[]{:S(2)}) copy-start(bf16[2048,768]{0,1:T(8,128)(2,1)} %copy-done.13) | copy-start | bytes 9437188
  642.3 33.7 %copy-start.2 = (f32[2048,768]{0,1:T(8,128)}, f32[2048,768]{0,1:T(8,128)S(1)}, u32[]{:S(2)}) copy-start(f32[2048,768]{0,1:T(8,128)S(1)} %get-tuple-element.69) | copy-start | bytes 18874372
  676.0 14.8 copy-start.34
  676.0 14.9 copy-start.36
  728.9 15.2 copy-start.31
  728.9 15.2 copy-start.33
  744.1 32.6 %copy-start.1 = (f32[2048,768]{0,1:T(8,128)}, f32[2048,768]{0,1:T(8,128)S(1)}, u32[]{:S(2)}) copy-start(f32[2048,768]{0,1:T(8,128)S(1)} %get-tuple-element.73) | copy-start | bytes 18874372
  776.7 16.8 %copy-start.10 = (bf16[2048,768]{0,1:T(8,128)(2,1)S(1)}, bf16[2048,768]{0,1:T(8,128)(2,1)}, u32[]{:S(2)}) copy-start(bf16[2048,768]{0,1:T(8,128)(2,1)} %copy-done.9) | copy-start | bytes 9437188
  776.7 16.9 %copy-start.28 = (f32[2048]{0:T(1024)S(1)}, f32[2048]{0:T(1024)}, u32[]{:S(2)}) copy-start(f32[2048]{0:T(1024)} %get-tuple-element.22) | copy-start | bytes 24580
  776.7 16.9 %copy-start.30 = (f32[2048]{0:T(1024)S(1)}, f32[2048]{0:T(1024)}, u32[]{:S(2)}) copy-start(f32[2048]{0:T(1024)} %copy-done.29) | copy-start | bytes 24580
  832.5 15.1 copy-start.23
  832.5 15.1 copy-start.25
  878.0 17.1 %copy-start.5 = (bf16[2048,768]{0,1:T(8,128)(2,1)S(1)}, bf16[2048,768]{0,1:T(8,128)(2,1)}, u32[]{:S(2)}) copy-start(bf16[2048,768]{0,1:T(8,128)(2,1)} %copy-done.4) | copy-start | bytes 9437188
  878.0 17.2 %copy-start.20 = (f32[2048]{0:T(1024)S(1)}, f32[2048]{0:T(1024)}, u32[]{:S(2)}) copy-start(f32[2048]{0:T(1024)} %get-tuple-element.18) | copy-start | bytes 24580
  878.0 17.2 %copy-start.22 = (f32[2048]{0:T(1024)S(1)}, f32[2048]{0:T(1024)}, u32[]{:S(2)}) copy-start(f32[2048]{0:T(1024)} %copy-done.21) | copy-start | bytes 24580
  927.7 279.4 %all-to-all-start.4 = ((f32[8,1024,768]{2,1,0:T(8,128)}), f32[8,1024,768]{2,1,0:T(8,128)}, u32[]{:S(2)}, u32[]{:S(2)}) async-start(f32[8,1024,768]{2,1,0:T(8,128)} %bitcast.315), calls=%async_computation.4 | async-start | bytes 50331648 | tf_op jit(solution)/shard_map/all_to_all | solution.py:121
  1207.1 279.4 %all-to-all-start.5 = ((f32[8,1024,768]{2,1,0:T(8,128)}), f32[8,1024,768]{2,1,0:T(8,128)}, u32[]{:S(2)}, u32[]{:S(2)}) async-start(f32[8,1024,768]{2,1,0:T(8,128)} %bitcast.314), calls=%async_computation.5 | async-start | bytes 50331648 | tf_op jit(solution)/shard_map/all_to_all | solution.py:121
  (13 other events, 45.7 us)
where the time goes:
time: 1590 us; the launch traced here: 1580 us
  matrix products  604 us (38%)
  waiting for transfers between devices  466 us (29%)
  other arithmetic  271 us (17%)
  local copies, waits for them, and re-layouts  211 us (13%)
  starting transfers between devices  26.6 us (2%)
    all_to_all x2, waiting for transfers between devices, return_rows(): recv_grad = lax.all_to_all(send_grad, 'emb', 0, 0, tiled=True)  431 us
    dot_general x6, matrix products, stack_backward(): jnp.einsum('td,fd->tf', d_low, w_down[layer_idx], preferred_element_type=...  190 us
    dot_general x8, matrix products, stack_forward(): jnp.dot(activated, w_down[layer_idx], preferred_element_type=jnp.float32)  175 us
    scatter-add x2, other arithmetic, return_rows(): return jax.ops.segment_sum(recv_grad, local_ids, num_segments=rows_dev)  130 us
    dot_general x6, matrix products, stack_backward(): jnp.einsum('tf,df->td', d_hid.astype(jnp.bfloat16), w_up[layer_idx], pref...  95.4 us
    dot_general x6, matrix products, stack_forward(): jnp.dot(normed, w_up[layer_idx], preferred_element_type=jnp.float32)  90 us
    gather x2, local copies, waits for them, and re-layouts, fetch_rows(): served = tables[which][local_ids]  84.4 us
    scatter x2, other arithmetic, return_rows(): jnp.zeros((n_dev * capacity, row_width), jnp.float32).at[dest_slot]  43.2 us
  transfers between devices with their start and end apart: 6, of which 3 were waited for; matrix products, arithmetic and copies ran while one was open for 38% of the time, Pallas kernels for 0%

commit v1 on v0

v1 whole, which is shorter than its diff:
```python
import functools

import jax
import jax.numpy as jnp
from jax import lax
from jax.experimental import pallas as pl
from jax.experimental.pallas import tpu as pltpu
from jax.sharding import PartitionSpec as P

EPS = 1e-6
GELU_K = 0.7978845608028654
GELU_C = 0.044715
F32 = jnp.float32
BF16 = jnp.bfloat16
UNIT = 16
LANE = 128
MAIN = 128
OVER = 384
NT = (((1,), (1,)), ((), ()))
NN = (((1,), (0,)), ((), ()))


def dot(a, b, dims=NN):
    return lax.dot_general(a, b, dims, preferred_element_type=F32)


def gelu(v):
    return v * (0.5 * (1.0 + jnp.tanh(GELU_K * (v + GELU_C * (v * v * v)))))


def gelu_grad(v):
    sq = v * v
    th = jnp.tanh(GELU_K * v * (1.0 + GELU_C * sq))
    return 0.5 * (1.0 + th) + (0.5 * v) * (1.0 - th * th) * (GELU_K + (3.0 * GELU_K * GELU_C) * sq)


def params(mb, sem=None):
    return pltpu.CompilerParams(vmem_limit_bytes=mb * 1024 * 1024, dimension_semantics=sem)


def cost(flops, nbytes):
    return pl.CostEstimate(flops=int(flops), bytes_accessed=int(nbytes), transcendentals=0)


def fwd_body(n_lay, tile, chunk, save_h, x0_ref, up_ref, dn_ref, gate_ref, *rest):
    if save_h:
        x_out, h_out, m_out, a_out, x_sc = rest
    else:
        x_out, m_out, a_out, x_sc = rest
    lay, blk = pl.program_id(0), pl.program_id(1)
    rows = pl.ds(pl.multiple_of(blk * tile, tile), tile)

    @pl.when(lay == 0)
    def _():
        x_sc[rows, :] = x0_ref[...]

    x_bf = x_sc[rows, :]
    x_out[0] = x_bf
    x_f = x_bf.astype(F32)
    inv = lax.rsqrt(jnp.mean(x_f * x_f, axis=-1, keepdims=True) + EPS)
    u = (x_f * inv).astype(BF16)
    acc = None
    for lo in range(0, up_ref.shape[2], chunk):
        h = dot(u, up_ref[0, :, lo:lo + chunk]).astype(BF16)
        if save_h:
            h_out[0, :, lo:lo + chunk] = h
        act = gelu(h.astype(F32)).astype(BF16)
        part = dot(act, dn_ref[0, lo:lo + chunk, :])
        acc = part if acc is None else acc + part
    m = acc.astype(BF16)

    @pl.when(lay < n_lay - 1)
    def _():
        x_sc[rows, :] = (x_f + m.astype(F32)).astype(BF16)

    @pl.when(lay == n_lay - 1)
    def _():
        m_out[...] = m
        a_out[...] = dot(u, gate_ref[0]).astype(BF16)


def fwd_layers(x0, w_up, w_down, w_gate, first, n_lay, table, save_h, tile=512, chunk=1024):
    n_tok, dim = x0.shape
    ff = w_up.shape[2]
    last = n_lay - 1
    in_specs = [
        pl.BlockSpec((tile, dim), lambda l, t: (jnp.where(l == 0, t, n_tok // tile - 1), 0)),
        pl.BlockSpec((1, dim, ff), lambda l, t: (first + l, 0, 0)),
        pl.BlockSpec((1, ff, dim), lambda l, t: (first + l, 0, 0)),
        pl.BlockSpec((1, dim, dim), lambda l, t: (table, 0, 0)),
    ]
    end = pl.BlockSpec((tile, dim), lambda l, t: (jnp.where(l == last, t, 0), 0))
    out_specs = [pl.BlockSpec((1, tile, dim), lambda l, t: (l, t, 0))]
    out_shape = [jax.ShapeDtypeStruct((n_lay, n_tok, dim), BF16)]
    if save_h:
        out_specs.append(pl.BlockSpec((1, tile, ff), lambda l, t: (l, t, 0)))
        out_shape.append(jax.ShapeDtypeStruct((n_lay, n_tok, ff), BF16))
    out_specs += [end, end]
    out_shape += [jax.ShapeDtypeStruct((n_tok, dim), BF16)] * 2
    return pl.pallas_call(
        functools.partial(fwd_body, n_lay, tile, chunk, save_h),
        grid=(n_lay, n_tok // tile), in_specs=in_specs, out_specs=out_specs, out_shape=out_shape,
        scratch_shapes=[pltpu.VMEM((n_tok, dim), BF16)],
        compiler_params=params(60, ("arbitrary", "arbitrary")),
        cost_estimate=cost(n_lay * 4 * n_tok * dim * ff, n_lay * (4 * dim * ff + 2 * n_tok * ff)),
        name=f"fwd_{first}",
    )(x0, w_up, w_down, w_gate)


def bwd_body(n_lay, tile, chunk, c0_ref, x_ref, h_ref, up_ref, dn_ref, da_ref, gate_ref, cb_out, c_sc, du_sc):
    step, blk = pl.program_id(0), pl.program_id(1)
    rows = pl.ds(pl.multiple_of(blk * tile, tile), tile)

    @pl.when(step == 0)
    def _():
        c_sc[rows, :] = c0_ref[...].astype(F32)

    c_b = c_sc[rows, :].astype(BF16)
    acc = None
    for lo in range(0, up_ref.shape[2], chunk):
        d_act = dot(c_b, dn_ref[0, lo:lo + chunk, :], NT)
        d_h = (gelu_grad(h_ref[0, :, lo:lo + chunk].astype(F32)) * d_act).astype(BF16)
        part = dot(d_h, up_ref[0, :, lo:lo + chunk], NT)
        acc = part if acc is None else acc + part
    du_sc[...] = acc

    @pl.when(step == 0)
    def _():
        du_sc[...] += dot(da_ref[...], gate_ref[0], NT)

    x_f = x_ref[0].astype(F32)
    inv = lax.rsqrt(jnp.mean(x_f * x_f, axis=-1, keepdims=True) + EPS)
    du = du_sc[...]
    c_new = c_sc[rows, :] + (inv * du - x_f * (inv * inv * inv) * jnp.mean(x_f * du, axis=-1, keepdims=True))
    c_sc[rows, :] = c_new

    @pl.when(step == n_lay - 1)
    def _():
        cb_out[...] = c_new.astype(BF16)


def bwd_layers(c0, x_all, h_all, w_up, w_down, d_gate, w_gate, last_layer, table, tile=512, chunk=1024):
    n_lay, n_tok, dim = x_all.shape
    ff = w_up.shape[2]
    end_blk = n_tok // tile - 1
    first_only = pl.BlockSpec((tile, dim), lambda i, t: (jnp.where(i == 0, t, end_blk), 0))
    return pl.pallas_call(
        functools.partial(bwd_body, n_lay, tile, chunk),
        grid=(n_lay, n_tok // tile),
        in_specs=[
            first_only,
            pl.BlockSpec((1, tile, dim), lambda i, t: (n_lay - 1 - i, t, 0)),
            pl.BlockSpec((1, tile, ff), lambda i, t: (n_lay - 1 - i, t, 0)),
            pl.BlockSpec((1, dim, ff), lambda i, t: (last_layer - i, 0, 0)),
            pl.BlockSpec((1, ff, dim), lambda i, t: (last_layer - i, 0, 0)),
            first_only,
            pl.BlockSpec((1, dim, dim), lambda i, t: (table, 0, 0)),
        ],
        out_specs=pl.BlockSpec((tile, dim), lambda i, t: (jnp.where(i == n_lay - 1, t, 0), 0)),
        out_shape=jax.ShapeDtypeStruct((n_tok, dim), BF16),
        scratch_shapes=[pltpu.VMEM((n_tok, dim), F32), pltpu.VMEM((tile, dim), F32)],
        compiler_params=params(60, ("arbitrary", "arbitrary")),
        cost_estimate=cost(n_lay * 4 * n_tok * dim * ff, n_lay * (4 * dim * ff + 2 * n_tok * ff)),
        name="bwd",
    )(c0, x_all, h_all, w_up, w_down, d_gate, w_gate)


def mix_body(want_e, n_main, n_over, blk, extra_ref, ids_ref, slots_ref, main_ref, over_ref, more_ref, x_ref, m_ref, a_ref, proj_ref, x_out, *rest):
    if want_e:
        e_out, acc = rest
    else:
        (acc,) = rest
    keys = ids_ref[0]
    lo = n_main + n_over
    acc[...] = (dot((keys == slots_ref[0, :, :n_main]).astype(BF16), main_ref[...])
                + dot((keys == slots_ref[0, :, n_main:lo]).astype(BF16), over_ref[...]))

    @pl.loop(0, extra_ref[0])
    def _(i):
        at = pl.multiple_of(i * blk, blk)
        hit = (keys == slots_ref[0, :, pl.ds(lo + at, blk)]).astype(BF16)
        acc[...] += dot(hit, more_ref[pl.ds(at, blk), :])

    e_f = acc[...]
    g = gelu(a_ref[...].astype(F32)).astype(BF16).astype(F32)
    z = (g * e_f).astype(BF16)
    q = dot(z, proj_ref[0]).astype(BF16)
    x_out[...] = ((x_ref[0].astype(F32) + m_ref[...].astype(F32)) + q.astype(F32)).astype(BF16)
    if want_e:
        e_out[...] = e_f.astype(BF16)


def mix_rows(extra, ids, slots, main, over, more, x_all, m, a, w_proj, table, want_e, tile=512, blk=LANE):
    n_tok, dim = m.shape
    n_slot = slots.shape[2]
    last = x_all.shape[0] - 1
    tok = pl.BlockSpec((tile, dim), lambda t, *_: (t, 0))
    whole = lambda arr: pl.BlockSpec(arr.shape, lambda t, *_: (0, 0))
    outs = 2 if want_e else 1
    return pl.pallas_call(
        functools.partial(mix_body, want_e, main.shape[0], over.shape[0], blk),
        grid_spec=pltpu.PrefetchScalarGridSpec(
            num_scalar_prefetch=1, grid=(n_tok // tile,),
            in_specs=[
                pl.BlockSpec((1, tile, 1), lambda t, *_: (table, t, 0)),
                pl.BlockSpec((1, 1, n_slot), lambda t, *_: (table, 0, 0)),
                whole(main), whole(over), whole(more),
                pl.BlockSpec((1, tile, dim), lambda t, *_: (last, t, 0)),
                tok, tok,
                pl.BlockSpec((1, dim, dim), lambda t, *_: (table, 0, 0)),
            ],
            out_specs=[tok] * outs,
            scratch_shapes=[pltpu.VMEM((tile, dim), F32)],
        ),
        out_shape=[jax.ShapeDtypeStruct((n_tok, dim), BF16)] * outs,
        compiler_params=params(48, ("arbitrary",)),
        cost_estimate=cost(2 * n_tok * dim * (dim + 1408), 12 * n_tok * dim),
        name=f"mix_{table}",
    )(extra, ids, slots, main, over, more, x_all, m, a, w_proj)


def grad_body(steps, tile, want_da, extra_ref, ids_ref, slots_ref, c_ref, a_ref, proj_ref, *rest):
    if want_da:
        e_ref, main_out, over_out, more_out, da_out, hi_sc, mid_sc, lo_sc = rest
    else:
        main_out, over_out, more_out, hi_sc, mid_sc, lo_sc = rest
    step = pl.program_id(0)
    main_steps, more_blk = steps
    n_main, n_over = main_out.shape[0] * main_steps, over_out.shape[0]

    @pl.when(step == 0)
    def _():
        @pl.loop(0, c_ref.shape[0], step=tile)
        def _(lo):
            rows = pl.ds(pl.multiple_of(lo, tile), tile)
            dz = dot(c_ref[rows, :], proj_ref[0], NT)
            a_f = a_ref[rows, :].astype(F32)
            g = gelu(a_f).astype(BF16).astype(F32)
            if want_da:
                da_out[rows, :] = (gelu_grad(a_f) * (dz * e_ref[rows, :].astype(F32))).astype(BF16)
            grad = g * dz
            hi = grad.astype(BF16)
            left = grad - hi.astype(F32)
            mid = left.astype(BF16)
            hi_sc[rows, :] = hi
            mid_sc[rows, :] = mid
            lo_sc[rows, :] = (left - mid.astype(F32)).astype(BF16)

    def sums(first, size):
        hit = (slots_ref[0, pl.ds(first, size), :] == ids_ref[0]).astype(BF16)
        return (dot(hit, lo_sc[...]) + dot(hit, mid_sc[...])) + dot(hit, hi_sc[...])

    @pl.when(step < main_steps)
    def _():
        blk = main_out.shape[0]
        main_out[...] = sums(pl.multiple_of(step * blk, blk), blk)

    @pl.when(step == main_steps)
    def _():
        over_out[...] = sums(n_main, n_over)

    @pl.when((step > main_steps) & ((step - main_steps - 1) < extra_ref[0]))
    def _():
        more_out[...] = sums(pl.multiple_of(n_main + n_over + (step - main_steps - 1) * more_blk, more_blk), more_blk)


def grad_rows(extra, ids, slots, c_b, a, e, w_proj, table, n_main, n_over, tile=512, main_steps=2, more_blk=LANE):
    n_tok, dim = c_b.shape
    n_slot = slots.shape[1]
    n_more = n_slot - n_main - n_over
    want_da = e is not None
    whole = pl.BlockSpec((n_tok, dim), lambda s, *_: (0, 0))
    in_specs = [
        pl.BlockSpec((1, 1, n_tok), lambda s, *_: (table, 0, 0)),
        pl.BlockSpec((1, n_slot, 1), lambda s, *_: (table, 0, 0)),
        whole, whole,
        pl.BlockSpec((1, dim, dim), lambda s, *_: (table, 0, 0)),
    ]

    def more_at(s, extra_ref):
        return (jnp.clip(s - main_steps - 1, 0, jnp.maximum(extra_ref[0] - 1, 0)), 0)

    out_specs = [
        pl.BlockSpec((n_main // main_steps, dim), lambda s, *_: (jnp.minimum(s, main_steps - 1), 0)),
        pl.BlockSpec((n_over, dim), lambda s, *_: (0, 0)),
        pl.BlockSpec((more_blk, dim), more_at),
    ]
    out_shape = [jax.ShapeDtypeStruct((n, dim), F32) for n in (n_main, n_over, n_more)]
    args = [extra, ids, slots, c_b, a, w_proj]
    if want_da:
        in_specs.append(whole)
        out_specs.append(whole)
        out_shape.append(jax.ShapeDtypeStruct((n_tok, dim), BF16))
        args.append(e)
    return pl.pallas_call(
        functools.partial(grad_body, (main_steps, more_blk), tile, want_da),
        grid_spec=pltpu.PrefetchScalarGridSpec(
            num_scalar_prefetch=1, grid=(main_steps + 1 + n_more // more_blk,), in_specs=in_specs, out_specs=out_specs,
            scratch_shapes=[pltpu.VMEM((n_tok, dim), BF16)] * 3,
        ),
        out_shape=out_shape,
        compiler_params=params(60, ("arbitrary",)),
        cost_estimate=cost(2 * n_tok * dim * (dim + 3 * 1408), 12 * n_tok * dim),
        name=f"grad_{table}",
    )(*args)


def local_row(key, base, rows_dev):
    row = key - base
    return jnp.where((row >= 0) & (row < rows_dev), row, rows_dev)


def unflatten(flat_sc, tab_ref, rows_dev, parts):
    @pl.loop(0, rows_dev // UNIT)
    def _(i):
        block = tab_ref[0, pl.ds(pl.multiple_of(i * UNIT, UNIT), UNIT), :].astype(F32)
        for p in range(parts):
            flat_sc[pl.ds(i * (UNIT * parts) + p, UNIT, stride=parts), :] = block[:, p * LANE:(p + 1) * LANE]


def pick_unit(slots_ref, src, at, base, rows_dev, parts, flat_sc, stage_sc, out_ref, to):
    for k in range(UNIT):
        row = local_row(slots_ref[src, at + k], base, rows_dev)
        stage_sc[k * parts:(k + 1) * parts, :] = flat_sc[pl.ds(row * parts, parts), :]
    rows = pl.ds(pl.multiple_of(to, UNIT), UNIT)
    for p in range(parts):
        out_ref[rows, p * LANE:(p + 1) * LANE] = stage_sc[pl.ds(p, UNIT, stride=parts), :].astype(BF16)


def serve_body(n_dev, rows_dev, parts, spans, meta_ref, slots_ref, tab_ref, *rest):
    outs, (flat_sc, stage_sc) = rest[:len(spans)], rest[len(spans):]
    me = meta_ref[0]
    base = me * rows_dev
    unflatten(flat_sc, tab_ref, rows_dev, parts)
    flat_sc[rows_dev * parts:(rows_dev + 1) * parts, :] = jnp.zeros((parts, LANE), F32)
    for out_ref, (first, size, direct) in zip(outs, spans):
        if not direct:
            @pl.loop(0, n_dev * size, step=UNIT)
            def _(i):
                out_ref[pl.ds(pl.multiple_of(i, UNIT), UNIT), :] = jnp.zeros((UNIT, parts * LANE), BF16)

        for src in range(n_dev):
            if direct:
                begin, end, at = 0, size // UNIT, first + me * size
            else:
                begin = jnp.clip((meta_ref[1 + src] - (first - n_dev * MAIN)) // UNIT, 0, size // UNIT)
                end = jnp.clip((meta_ref[1 + n_dev + src] - (first - n_dev * MAIN) + (UNIT - 1)) // UNIT, 0, size // UNIT)
                at = first

            @pl.loop(begin, end)
            def _(i):
                pick_unit(slots_ref, src, at + i * UNIT, base, rows_dev, parts, flat_sc, stage_sc, out_ref, src * size + i * UNIT)


def serve_rows(meta, slots_all, tables, table, n_dev, spans):
    _, rows_dev, dim = tables.shape
    parts = dim // LANE
    sizes = [n_dev * size for _, size, _ in spans]
    return pl.pallas_call(
        functools.partial(serve_body, n_dev, rows_dev, parts, spans),
        grid_spec=pltpu.PrefetchScalarGridSpec(
            num_scalar_prefetch=2, grid=(1,),
            in_specs=[pl.BlockSpec((1, rows_dev, dim), lambda i, *_: (table, 0, 0), pipeline_mode=pl.Buffered(1))],
            out_specs=[pl.BlockSpec((n, dim), lambda i, *_: (0, 0), pipeline_mode=pl.Buffered(1)) for n in sizes],
            scratch_shapes=[pltpu.VMEM(((rows_dev + 8) * parts, LANE), F32), pltpu.VMEM((UNIT * parts, LANE), F32)],
        ),
        out_shape=[jax.ShapeDtypeStruct((n, dim), BF16) for n in sizes],
        compiler_params=params(62, ("arbitrary",)),
        cost_estimate=cost(20e9, 22e6),
        name=f"serve_{table}",
    )(meta, slots_all, tables)


def collect_body(n_dev, rows_dev, parts, sizes, has_prev, meta_ref, slots_ref, main_ref, over_ref, more_ref, *rest):
    if has_prev:
        rest = rest[1:]
    out_ref, flat_sc, main_sc, over_sc, unit_sc, stage_sc, sems = rest
    step = pl.program_id(0)
    me = meta_ref[0]
    base = me * rows_dev
    n_main, n_over, n_more = sizes

    def part_copy(src, dst, i, n, sem):
        rows = pl.ds(i * n, n)
        return pltpu.make_async_copy(src.at[rows, :], dst.at[rows, :], sem)

    def add_unit(src, at, buf, rows):
        for p in range(parts):
            stage_sc[pl.ds(p, UNIT, stride=parts), :] = buf[rows, p * LANE:(p + 1) * LANE]
        where = [pl.ds(local_row(slots_ref[src, at + k], base, rows_dev) * parts, parts) for k in range(UNIT)]
        sums = [flat_sc[where[k], :] + stage_sc[k * parts:(k + 1) * parts, :] for k in range(UNIT)]
        for k in range(UNIT):
            flat_sc[where[k], :] = sums[k]

    def units(src, first, size):
        begin = jnp.clip((meta_ref[1 + src] - first) // UNIT, 0, size // UNIT)
        end = jnp.clip((meta_ref[1 + n_dev + src] - first + (UNIT - 1)) // UNIT, 0, size // UNIT)
        return begin, end

    @pl.when(step == 0)
    def _():
        for s in range(n_dev):
            part_copy(main_ref, main_sc, s, n_main, sems.at[s]).start()
            part_copy(over_ref, over_sc, s, n_over, sems.at[n_dev + s]).start()

        @pl.loop(0, rows_dev // 8)
        def _(i):
            flat_sc[pl.ds(pl.multiple_of(i * 8 * parts, 8), 8 * parts), :] = jnp.zeros((8 * parts, LANE), F32)

        for s in range(n_dev):
            part_copy(main_ref, main_sc, s, n_main, sems.at[s]).wait()

            @pl.loop(0, (meta_ref[1 + 2 * n_dev + s] + (UNIT - 1)) // UNIT)
            def _(i):
                add_unit(s, me * n_main + i * UNIT, main_sc, pl.ds(pl.multiple_of(s * n_main + i * UNIT, UNIT), UNIT))

        for s in range(n_dev):
            part_copy(over_ref, over_sc, s, n_over, sems.at[n_dev + s]).wait()

            @pl.loop(*units(s, 0, n_over))
            def _(i):
                add_unit(s, n_dev * n_main + i * UNIT, over_sc, pl.ds(pl.multiple_of(s * n_over + i * UNIT, UNIT), UNIT))

        for s in range(n_dev):
            @pl.loop(*units(s, n_over, n_more))
            def _(i):
                rows = pl.ds(pl.multiple_of(s * n_more + i * UNIT, UNIT), UNIT)
                copy = pltpu.make_async_copy(more_ref.at[rows, :], unit_sc, sems.at[2 * n_dev])
                copy.start()
                copy.wait()
                add_unit(s, n_dev * n_main + n_over + i * UNIT, unit_sc, pl.ds(0, UNIT))

    @pl.when(step > 0)
    def _():
        blk = out_ref.shape[1]
        first = (step - 1) * (blk * parts)

        @pl.loop(0, blk // 8)
        def _(i):
            to = pl.ds(pl.multiple_of(i * 8, 8), 8)
            for p in range(parts):
                out_ref[0, to, p * LANE:(p + 1) * LANE] = flat_sc[pl.ds(first + i * (8 * parts) + p, 8, stride=parts), :]


def collect_rows(meta, slots_all, main, over, more, prev, table, n_tables, rows_dev, n_dev, n_blk=6):
    dim = main.shape[1]
    parts = dim // LANE
    blk = rows_dev // n_blk
    any_spec = pl.BlockSpec(memory_space=pl.ANY)
    args = [meta, slots_all, main, over, more]
    alias = {}
    if prev is not None:
        args.append(prev)
        alias = {5: 0}
    return pl.pallas_call(
        functools.partial(collect_body, n_dev, rows_dev, parts, [r.shape[0] // n_dev for r in (main, over, more)], prev is not None),
        grid_spec=pltpu.PrefetchScalarGridSpec(
            num_scalar_prefetch=2, grid=(1 + n_blk,), in_specs=[any_spec] * (len(args) - 2),
            out_specs=pl.BlockSpec((1, blk, dim), lambda i, *_: (table, jnp.maximum(i - 1, 0), 0)),
            scratch_shapes=[
                pltpu.VMEM(((rows_dev + 8) * parts, LANE), F32),
                pltpu.VMEM(main.shape, F32),
                pltpu.VMEM(over.shape, F32),
                pltpu.VMEM((UNIT, dim), F32),
                pltpu.VMEM((UNIT * parts, LANE), F32),
                pltpu.SemaphoreType.DMA((2 * n_dev + 1,)),
            ],
        ),
        out_shape=jax.ShapeDtypeStruct((n_tables, rows_dev, dim), F32),
        input_output_aliases=alias,
        compiler_params=params(56, ("arbitrary",)),
        cost_estimate=cost(20e9, 30e6),
        name=f"collect_{table}",
    )(*args)


def blank(shape, dtype):
    return pl.pallas_call(lambda o: None, out_specs=pl.BlockSpec(memory_space=pl.ANY),
                          out_shape=jax.ShapeDtypeStruct(shape, dtype), name="blank")()


def layout_body(n_dev, cnt_ref, uniq_ref, out_ref):
    n_tab, _, n = uniq_ref.shape
    n_main = n_dev * MAIN
    lane = lax.broadcasted_iota(jnp.int32, (1, n), 1)
    small = lax.broadcasted_iota(jnp.int32, (1, MAIN), 1)
    for j in range(n_tab):
        uniq = uniq_ref[j]
        over = jnp.full((1, n), -1, jnp.int32)
        tail = jnp.zeros((1, LANE), jnp.int32)
        start = jnp.int32(0)
        at = jnp.int32(0)
        for o in range(n_dev):
            cnt = cnt_ref[j, o]
            head = pltpu.roll(uniq, lax.rem(n - start, n), 1)[:, :MAIN]
            out_ref[j, :, o * MAIN:(o + 1) * MAIN] = jnp.where(small < cnt, head, -1)
            extra = jnp.maximum(cnt - MAIN, 0)
            moved = pltpu.roll(uniq, lax.rem(2 * n + at - start - MAIN, n), 1)
            over = jnp.where((lane >= at) & (lane < at + extra), moved, over)
            tail = jnp.where(lax.broadcasted_iota(jnp.int32, (1, LANE), 1) == o, cnt, tail)
            start = start + cnt
            at = at + extra
        out_ref[j, :, n_main:n_main + n] = over
        out_ref[j, :, n_main + n:] = tail


def route(ids, rows_dev, n_dev):
    n_tab, n_tok = ids.shape
    ordered = lax.sort(ids, dimension=1)
    first = jnp.concatenate([jnp.ones((n_tab, 1), bool), ordered[:, 1:] != ordered[:, :-1]], axis=1)
    lo = (jnp.arange(n_dev, dtype=jnp.int32) * rows_dev)[None, :, None]
    mine = first[:, None, :] & (ordered[:, None, :] >= lo) & (ordered[:, None, :] < lo + rows_dev)
    counts = jnp.sum(mine.astype(jnp.int32), axis=2)
    uniq = lax.sort(jnp.where(first, ordered, jnp.int32(2 ** 30)), dimension=1)
    return pl.pallas_call(
        functools.partial(layout_body, n_dev),
        grid_spec=pltpu.PrefetchScalarGridSpec(
            num_scalar_prefetch=1, grid=(1,),
            in_specs=[pl.BlockSpec((n_tab, 1, n_tok), lambda i, *_: (0, 0, 0))],
            out_specs=pl.BlockSpec((n_tab, 1, n_dev * MAIN + n_tok + LANE), lambda i, *_: (0, 0, 0))),
        out_shape=jax.ShapeDtypeStruct((n_tab, 1, n_dev * MAIN + n_tok + LANE), jnp.int32),
        name="layout",
    )(counts, uniq.reshape(n_tab, 1, n_tok))


def solution(mesh):
    n_dev = mesh.shape['emb']
    tok_spec = P('emb', None)
    tab_spec = P(None, 'emb', None)

    def local_program(x_start, d_out, token_ids, w_up, w_down, w_gate, w_proj, tables):
        n_tab, n_tok = token_ids.shape[:2]
        rows_dev, dim = tables.shape[1:]
        layers = w_up.shape[0]
        me = lax.axis_index('emb').astype(jnp.int32)
        ids = token_ids.reshape(n_tab, n_tok)
        sent = route(ids, rows_dev, n_dev)
        n_main, n_over, n_more = n_dev * MAIN, OVER, n_tok - OVER
        n_slot = n_main + n_tok
        got = lax.all_gather(sent[:, 0], 'emb')
        counts = got[:, :, n_slot:n_slot + n_dev]
        extra = jnp.maximum(counts - MAIN, 0)
        starts = jnp.cumsum(extra, axis=2) - extra
        rest = jnp.sum(extra, axis=2)
        ids_col, ids_row = token_ids, ids.reshape(n_tab, 1, n_tok)
        slots_row = sent[:, :, :n_slot]
        slots_col = slots_row.reshape(n_tab, n_slot, 1)
        plan = []
        for j in range(n_tab):
            to_me = lambda a: lax.dynamic_index_in_dim(a[:, j], me, axis=1, keepdims=False)
            begin = to_me(starts)
            meta = jnp.concatenate([me[None], begin, begin + to_me(extra), jnp.minimum(to_me(counts), MAIN)])
            mine = lax.dynamic_index_in_dim(rest[:, j], me, axis=0, keepdims=True)
            more = jnp.maximum(mine - OVER + (LANE - 1), 0) // LANE
            plan.append(dict(meta=meta, slots=got[:, j, :n_slot], more=more, spill=jnp.any(rest[:, j] > OVER)))

        def fetch(j):
            p = plan[j]
            main, over = serve_rows(p['meta'], p['slots'], tables, j, n_dev, ((0, MAIN, True), (n_main, OVER, False)))
            main = lax.all_to_all(main, 'emb', 0, 0, tiled=True)
            over = lax.psum_scatter(over, 'emb', scatter_dimension=0, tiled=True)

            def all_rows():
                (more,) = serve_rows(p['meta'], p['slots'], tables, j, n_dev, ((n_main + OVER, n_more, False),))
                return lax.psum_scatter(more, 'emb', scatter_dimension=0, tiled=True)

            more = lax.cond(p['spill'], all_rows, lambda: blank((n_more, dim), BF16))
            return main, over, more

        def give_back(j, main, over, more):
            main = lax.all_to_all(main, 'emb', 0, 0, tiled=True)
            over = lax.all_gather(over, 'emb', axis=0, tiled=True)
            more = lax.cond(plan[j]['spill'], lambda: lax.all_gather(more, 'emb', axis=0, tiled=True),
                            lambda: blank((n_dev * n_more, dim), F32))
            return main, over, more

        def collect(j, received, prev):
            return collect_rows(plan[j]['meta'], plan[j]['slots'], *received, prev, j, n_tab, rows_dev, n_dev)

        rows_0 = fetch(0)
        rows_1 = fetch(1)
        x_a, m_a, a_0 = fwd_layers(x_start, w_up, w_down, w_gate, 0, 2, 0, False)
        (x_2,) = mix_rows(plan[0]['more'], ids_col, slots_row, *rows_0, x_a, m_a, a_0, w_proj, 0, False)
        x_b, h_b, m_b, a_1 = fwd_layers(x_2, w_up, w_down, w_gate, 2, layers - 2, 1, True)
        x_end, e_1 = mix_rows(plan[1]['more'], ids_col, slots_row, *rows_1, x_b, m_b, a_1, w_proj, 1, True)
        *sums_1, d_a = grad_rows(plan[1]['more'], ids_row, slots_col, d_out, a_1, e_1, w_proj, 1, n_main, n_over)
        recv_1 = give_back(1, *sums_1)
        c_b = bwd_layers(d_out, x_b, h_b, w_up, w_down, d_a, w_gate, layers - 1, 1)
        sums_0 = grad_rows(plan[0]['more'], ids_row, slots_col, c_b, a_0, None, w_proj, 0, n_main, n_over)
        recv_0 = give_back(0, *sums_0)
        grads = collect(0, recv_0, collect(1, recv_1, None))
        return x_end, grads

    return jax.shard_map(local_program, mesh=mesh, in_specs=(tok_spec, tok_spec, tab_spec, P(), P(), P(), P(), tab_spec), out_specs=(tok_spec, tab_spec), check_vma=False)
```

time: 1590 us -> 811 us (0.51)
  the two profiles are of different devices: /device:TPU:0 before, /device:TPU:3 now
where the time goes in v1:
time: 811 us; the launch traced here: 803 us
  Pallas kernels  579 us (71%)
  waiting for transfers between devices  94 us (12%)
  blocking collectives  62 us (8%)
  local copies, waits for them, and re-layouts  25.6 us (3%)
  between operations  17.2 us (2%)
  starting transfers between devices  16.2 us (2%)
  other arithmetic  8.29 us (1%)
    pallas_call x2, Pallas kernels, fwd_layers(): pl.pallas_call(functools.partial(fwd_body, n_lay, tile, chunk, save_h), g...  212 us
    pallas_call x1, Pallas kernels, bwd_layers(): pl.pallas_call(functools.partial(bwd_body, n_lay, tile, chunk), grid=(n_l...  181 us
    all_gather x2, waiting for transfers between devices, give_back(): over = lax.all_gather(over, 'emb', axis=0, tiled=True)  92.7 us
    pallas_call x2, Pallas kernels, grad_rows(): pl.pallas_call(functools.partial(grad_body, (main_steps, more_blk), tile,...  58.5 us
    all_to_all x1, blocking collectives, give_back(): main = lax.all_to_all(main, 'emb', 0, 0, tiled=True)  51.7 us
    pallas_call x2, Pallas kernels, collect_rows(): pl.pallas_call(functools.partial(collect_body, n_dev, rows_dev, parts, [r...  50.8 us
    pallas_call x2, Pallas kernels, serve_rows(): pl.pallas_call(functools.partial(serve_body, n_dev, rows_dev, parts, span...  44.3 us
    pallas_call x2, Pallas kernels, mix_rows(): pl.pallas_call(functools.partial(mix_body, want_e, main.shape[0], over.sh...  30.7 us
  transfers between devices with their start and end apart: 7, of which 2 were waited for; matrix products, arithmetic and copies ran while one was open for 1% of the time, Pallas kernels for 33%

profile of v1, /device:TPU:3, one launch (start us, length us, event | category | flops | bytes accessed | tf_op | source)
XLA Modules:
  0.0 802.8 jit_solution(4006037509648852029)
XLA Ops:
  7.2 1.3 copy.53
  8.6 8.1 %sort.17.cloned.1.call-done = s32[2,2048]{1,0:T(2,128)} async-done(((s32[2,2048]{1,0:T(2,128)}), s32[2,2048]{1,0:T(2,128)}) %sort.17.cloned.1.call-update) | async-done | bytes 16400 | tf_op jit(solution)/shard_map/sort | solution.py:509
  16.7 0.9 slice_compare_fusion
  17.7 1.4 broadcast_select_fusion
  19.1 1.5 convert_reduce_fusion.cnt_ref
  20.7 6.2 sort.19.cloned.1.call-done
  26.9 1.3 reshape.90.uniq_ref
  28.2 2.8 layout.1
  31.0 10.3 %all-gather = s32[16,1,3200]{2,1,0:T(1,128)S(1)} all-gather(s32[2,1,3200]{2,1,0:T(1,128)} %layout.1), channel_id=2, replica_groups=mesh['emb'=8] {'emb'}, dimensions={0}, use_global_device_ids=true | all-gather | bytes 230400 | tf_op jit(solution)/shard_map/all_gather | solution.py:540
  41.9 1.4 reduce_window_sum.11
  44.8 26.4 %serve_0.3 = (bf16[1024,768]{1,0:T(8,128)(2,1)}, bf16[3072,768]{1,0:T(8,128)(2,1)}) custom-call(s32[25]{0:T(128)S(1)} %pad_add_fusion.1.meta_ref, s32[8,3072]{1,0:T(8,128)S(1)} %bitcast.28, bf16[2,6288,768]{2,1,0:T(8,128)(2,1)} %tab_ref.3), custom_call_target="tpu_custom_call" | custom-call | flops 20000000000 | bytes 22000000 | tf_op jit(solution)/shard_map/serve_0/pallas_call | solution.py:359
  71.2 0.7 compare_reduce_fusion
  74.6 1.9 copy.39.ids_ref
  76.5 55.9 %fwd_0.1 = (bf16[2,2048,768]{2,1,0:T(8,128)(2,1)}, bf16[2048,768]{1,0:T(8,128)(2,1)}, bf16[2048,768]{1,0:T(8,128)(2,1)}) custom-call(bf16[2048,768]{1,0:T(8,128)(2,1)} %x0_ref.1, bf16[8,768,3072]{2,1,0:T(8,128)(2,1)} %up_ref.5, bf16[8,3072,768]{2,1,0:T(8,128)(2,1)} %dn_ref.5, bf16[2,768,768]{2,1,0:T(8,128)(2,1)} %gate_ref.5), custom_call_target="tpu_custom_call" | custom-call | flops 38654705664 | bytes 44040192 | tf_op jit(solution)/shard_map/fwd_0/pallas_call | solution.py:100
  134.4 2.7 reshape.95.slots_ref
  137.1 3.0 all-to-all-start.1
  140.1 17.9 %serve_1.3 = (bf16[1024,768]{1,0:T(8,128)(2,1)}, bf16[3072,768]{1,0:T(8,128)(2,1)}) custom-call(s32[25]{0:T(128)S(1)} %pad_add_fusion.meta_ref, s32[8,3072]{1,0:T(8,128)S(1)} %bitcast.32, bf16[2,6288,768]{2,1,0:T(8,128)(2,1)} %tab_ref.3), custom_call_target="tpu_custom_call" | custom-call | flops 20000000000 | bytes 22000000 | tf_op jit(solution)/shard_map/serve_1/pallas_call | solution.py:359
  158.0 8.2 %all-to-all-start = ((bf16[8,128,768]{2,1,0:T(8,128)(2,1)}), bf16[8,128,768]{2,1,0:T(8,128)(2,1)}, u32[]{:S(2)}, u32[]{:S(2)}) async-start(bf16[8,128,768]{2,1,0:T(8,128)(2,1)} %bitcast.27), calls=%async_computation.2 | async-start | bytes 3145728 | tf_op jit(solution)/shard_map/all_to_all | solution.py:560
  166.3 1.1 copy-done.2
  167.4 15.3 %mix_0.1.x0_ref = bf16[2048,768]{1,0:T(8,128)(2,1)} custom-call(s32[1]{0:T(128)S(6)} %select_n.27.extra_ref, s32[2,2048,1]{2,1,0:T(8,128)S(1)} %copy-done, s32[2,1,3072]{2,1,0:T(1,128)S(1)} %get-tuple-element.83.slots_ref, bf16[1024,768]{1,0:T(8,128)(2,1)} %bitcast.10.main_ref, bf16[384,768]{1,0:T(8,128)(2,1)S(1)} %copy-done.2, ...), custom_call_target="tpu_custom_call" | custom-call | flops 6845104128 | bytes 18874368 | tf_op jit(solution)/shard_map/mix_0/pallas_call | solution.py:200
  182.7 155.8 %fwd_2.1 = (bf16[6,2048,768]{2,1,0:T(8,128)(2,1)}, bf16[6,2048,3072]{2,1,0:T(8,128)(2,1)}, bf16[2048,768]{1,0:T(8,128)(2,1)}, bf16[2048,768]{1,0:T(8,128)(2,1)}) custom-call(bf16[2048,768]{1,0:T(8,128)(2,1)} %mix_0.1.x0_ref, bf16[8,768,3072]{2,1,0:T(8,128)(2,1)} %up_ref.5, bf16[8,3072,768]{2,1,0:T(8,128)(2,1)} %dn_ref.5, bf16[2,768,768]{2,1,0:T(8,128)(2,1)} %gate_ref.5), custom_call_target="tpu_custom_call" | custom-call | flops 115964116992 | bytes 132120576 | tf_op jit(solution)/shard_map/fwd_2/pallas_call | solution.py:100
  338.6 1.1 copy-done.1
  339.6 15.4 %mix_1.1 = (bf16[2048,768]{1,0:T(8,128)(2,1)}, bf16[2048,768]{1,0:T(8,128)(2,1)}) custom-call(s32[1]{0:T(128)S(6)} %select_n.26.extra_ref, s32[2,2048,1]{2,1,0:T(8,128)S(1)} %copy-done, s32[2,1,3072]{2,1,0:T(1,128)S(1)} %get-tuple-element.83.slots_ref, bf16[1024,768]{1,0:T(8,128)(2,1)} %bitcast.5.main_ref, bf16[384,768]{1,0:T(8,128)(2,1)S(1)} %copy-done.1, ...), custom_call_target="tpu_custom_call" | custom-call | flops 6845104128 | bytes 18874368 | tf_op jit(solution)/shard_map/mix_1/pallas_call | solution.py:200
  355.0 32.3 %grad_1.1 = (f32[1024,768]{1,0:T(8,128)}, f32[384,768]{1,0:T(8,128)}, f32[1664,768]{1,0:T(8,128)}, bf16[2048,768]{1,0:T(8,128)(2,1)}) custom-call(s32[1]{0:T(128)S(6)} %select_n.26.extra_ref, s32[2,1,2048]{2,1,0:T(1,128)} %bitcast.34, s32[2,3072,1]{2,1,0:T(8,128)} %reshape.95.slots_ref, bf16[2048,768]{1,0:T(8,128)(2,1)} %c0_ref.1, ...), custom_call_target="tpu_custom_call" | custom-call | flops 15703474176 | bytes 18874368 | tf_op jit(solution)/shard_map/grad_1/pallas_call | solution.py:295
  387.3 180.7 %bwd.1.c_ref = bf16[2048,768]{1,0:T(8,128)(2,1)} custom-call(bf16[2048,768]{1,0:T(8,128)(2,1)} %c0_ref.1, bf16[6,2048,768]{2,1,0:T(8,128)(2,1)} %get-tuple-element.61.x_ref, bf16[6,2048,3072]{2,1,0:T(8,128)(2,1)} %get-tuple-element.65.h_ref, bf16[8,768,3072]{2,1,0:T(8,128)(2,1)} %up_ref.5, bf16[8,3072,768]{2,1,0:T(8,128)(2,1)} %dn_ref.5, ...), custom_call_target="tpu_custom_call" | custom-call | flops 115964116992 | bytes 132120576 | tf_op jit(solution)/shard_map/bwd/pallas_call | solution.py:147
  568.0 26.2 %grad_0.1 = (f32[1024,768]{1,0:T(8,128)}, f32[384,768]{1,0:T(8,128)}, f32[1664,768]{1,0:T(8,128)}) custom-call(s32[1]{0:T(128)S(6)} %select_n.27.extra_ref, s32[2,1,2048]{2,1,0:T(1,128)} %bitcast.35, s32[2,3072,1]{2,1,0:T(8,128)} %reshape.95.slots_ref, bf16[2048,768]{1,0:T(8,128)(2,1)} %bwd.1.c_ref, bf16[2048,768]{1,0:T(8,128)(2,1)} %get-tuple-element.60.a_ref, ...), custom_call_target="tpu_custom_call" | custom-call | flops 15703474176 | bytes 18874368 | tf_op jit(solution)/shard_map/grad_0/pallas_call | solution.py:295
  596.1 51.7 %all_to_all.44 = f32[8,128,768]{2,1,0:T(8,128)} all-to-all(f32[8,128,768]{2,1,0:T(8,128)S(1)} %bitcast.26), channel_id=1, replica_groups=mesh['emb'=8] {'emb'}, dimensions={0} | all-to-all | bytes 6291456 | tf_op jit(solution)/shard_map/all_to_all | solution.py:571
  647.8 4.3 all-to-all-start.2
  652.1 58.6 %all-gather.12.cloned.1.call-done.over_ref = f32[3072,768]{1,0:T(8,128)} async-done(((f32[384,768]{1,0:T(8,128)}), f32[3072,768]{1,0:T(8,128)}) %all-gather.12.cloned.1.call-update) | async-done | bytes 9437200 | tf_op jit(solution)/shard_map/all_gather | solution.py:572
  710.7 20.5 %collect_1.1.rest_0_ = f32[2,6288,768]{2,1,0:T(8,128)} custom-call(s32[25]{0:T(128)S(1)} %copy-done.14, s32[8,3072]{1,0:T(8,128)S(1)} %bitcast.33, f32[1024,768]{1,0:T(8,128)} %bitcast.23, f32[3072,768]{1,0:T(8,128)} %all-gather.12.cloned.1.call-done.over_ref, f32[13312,768]{1,0:T(8,128)} %get-tuple-element.101.more_ref), custom_call_target="tpu_custom_call" | custom-call | flops 20000000000 | bytes 30000000 | tf_op jit(solution)/shard_map/collect_1/pallas_call | solution.py:455
  731.2 34.1 %all-gather.10.cloned.1.call-done.over_ref = f32[3072,768]{1,0:T(8,128)} async-done(((f32[384,768]{1,0:T(8,128)}), f32[3072,768]{1,0:T(8,128)}) %all-gather.10.cloned.1.call-update) | async-done | bytes 9437200 | tf_op jit(solution)/shard_map/all_gather | solution.py:572
  765.3 30.4 %collect_0.1 = f32[2,6288,768]{2,1,0:T(8,128)} custom-call(s32[25]{0:T(128)S(1)} %copy-done.12, s32[8,3072]{1,0:T(8,128)S(1)} %bitcast.30, f32[1024,768]{1,0:T(8,128)} %bitcast.24, f32[3072,768]{1,0:T(8,128)} %all-gather.10.cloned.1.call-done.over_ref, f32[13312,768]{1,0:T(8,128)} %get-tuple-element.100.more_ref, ...), custom_call_target="tpu_custom_call", output_to_operand_aliasing={{}: (5, {})} | custom-call | flops 20000000000 | bytes 30000000 | tf_op jit(solution)/shard_map/collect_0/pallas_call | solution.py:455
  (76 shorter events, 6.2 us)
Async XLA Ops:
  7.2 9.6 %sort.17.cloned.1.call-start = ((), (), s32[]{:S(2)}) async-start(), calls=%async_computation.16 | async-start | bytes 49184 | tf_op jit(solution)/shard_map/sort | solution.py:509
  8.6 18.3 %sort.19.cloned.1.call-start = ((), (), s32[]{:S(2)}) async-start(), calls=%async_computation.17 | async-start | bytes 49184 | tf_op jit(solution)/shard_map/sort | solution.py:514
  43.7 30.0 %copy-start.5 = (s32[8,1,3072]{2,0,1:T(8,128)}, s32[8,1,3072]{2,0,1:T(8,128)S(1)}, u32[]{:S(2)}) copy-start(s32[8,1,3072]{2,0,1:T(8,128)S(1)} %copy.51) | copy-start | bytes 294916
  44.7 29.0 %copy-start.11 = (s32[25]{0:T(128)}, s32[25]{0:T(128)S(1)}, u32[]{:S(2)}) copy-start(s32[25]{0:T(128)S(1)} %pad_add_fusion.1.meta_ref) | copy-start | bytes 304
  73.2 66.9 %copy-start.7 = (s32[8,1,3072]{2,0,1:T(8,128)}, s32[8,1,3072]{2,0,1:T(8,128)S(1)}, u32[]{:S(2)}) copy-start(s32[8,1,3072]{2,0,1:T(8,128)S(1)} %copy.52) | copy-start | bytes 294916
  73.8 66.4 %copy-start.13 = (s32[25]{0:T(128)}, s32[25]{0:T(128)S(1)}, u32[]{:S(2)}) copy-start(s32[25]{0:T(128)S(1)} %pad_add_fusion.meta_ref) | copy-start | bytes 304
  73.8 0.8 copy-start.10
  73.8 92.5 %reduce-scatter.11.cloned.1.call-start = ((), (), s32[]{:S(2)}) async-start(), calls=%async_computation.13 | async-start | bytes 5308416 | tf_op jit(solution)/shard_map/reduce_scatter | solution.py:561
  76.5 57.8 %copy-start.9 = (s32[2,1,3200]{2,1,0:T(1,128)S(1)}, s32[2,1,3200]{2,1,0:T(1,128)}, u32[]{:S(2)}) copy-start(s32[2,1,3200]{2,1,0:T(1,128)} %layout.1) | copy-start | bytes 76804
  137.1 21.0 %all-to-all-start.1 = ((bf16[8,128,768]{2,1,0:T(8,128)(2,1)}), bf16[8,128,768]{2,1,0:T(8,128)(2,1)}, u32[]{:S(2)}, u32[]{:S(2)}) async-start(bf16[8,128,768]{2,1,0:T(8,128)(2,1)} %bitcast.9), calls=%async_computation.4 | async-start | bytes 3145728 | tf_op jit(solution)/shard_map/all_to_all | solution.py:560
  140.0 198.5 %reduce-scatter.9.cloned.1.call-start = ((), (), s32[]{:S(2)}) async-start(), calls=%async_computation.12 | async-start | bytes 5308416 | tf_op jit(solution)/shard_map/reduce_scatter | solution.py:561
  158.0 8.3 %copy-start = (s32[2,2048,1]{2,1,0:T(8,128)S(1)}, s32[2,2048,1]{2,1,0:T(8,128)}, u32[]{:S(2)}) copy-start(s32[2,2048,1]{2,1,0:T(8,128)} %copy.39.ids_ref) | copy-start | bytes 49156
  158.0 180.5 %all-to-all-start = ((bf16[8,128,768]{2,1,0:T(8,128)(2,1)}), bf16[8,128,768]{2,1,0:T(8,128)(2,1)}, u32[]{:S(2)}, u32[]{:S(2)}) async-start(bf16[8,128,768]{2,1,0:T(8,128)(2,1)} %bitcast.27), calls=%async_computation.2 | async-start | bytes 3145728 | tf_op jit(solution)/shard_map/all_to_all | solution.py:560
  166.3 1.1 copy-start.2
  338.6 1.1 copy-start.1
  594.2 1.9 copy-start.4
  594.3 116.4 %all-gather.12.cloned.1.call-start = ((), (), s32[]{:S(2)}) async-start(), calls=%async_computation.15 | async-start | bytes 10616832 | tf_op jit(solution)/shard_map/all_gather | solution.py:572
  594.9 170.5 %all-gather.10.cloned.1.call-start = ((), (), s32[]{:S(2)}) async-start(), calls=%async_computation.14 | async-start | bytes 10616832 | tf_op jit(solution)/shard_map/all_gather | solution.py:572
  647.8 62.9 %copy-start.8 = (s32[8,1,3072]{2,0,1:T(8,128)S(1)}, s32[8,1,3072]{2,0,1:T(8,128)}, u32[]{:S(2)}) copy-start(s32[8,1,3072]{2,0,1:T(8,128)} %copy-done.7) | copy-start | bytes 294916
  647.8 62.9 %copy-start.14 = (s32[25]{0:T(128)S(1)}, s32[25]{0:T(128)}, u32[]{:S(2)}) copy-start(s32[25]{0:T(128)} %copy-done.13) | copy-start | bytes 304
  647.8 83.3 %all-to-all-start.2 = ((f32[8,128,768]{2,1,0:T(8,128)}), f32[8,128,768]{2,1,0:T(8,128)S(1)}, u32[]{:S(2)}, u32[]{:S(2)}) async-start(f32[8,128,768]{2,1,0:T(8,128)} %bitcast.25), calls=%async_computation.6 | async-start | bytes 6291456 | tf_op jit(solution)/shard_map/all_to_all | solution.py:571
  710.7 54.7 %copy-start.6 = (s32[8,1,3072]{2,0,1:T(8,128)S(1)}, s32[8,1,3072]{2,0,1:T(8,128)}, u32[]{:S(2)}) copy-start(s32[8,1,3072]{2,0,1:T(8,128)} %copy-done.5) | copy-start | bytes 294916
  710.7 54.7 %copy-start.12 = (s32[25]{0:T(128)S(1)}, s32[25]{0:T(128)}, u32[]{:S(2)}) copy-start(s32[25]{0:T(128)} %copy-done.11) | copy-start | bytes 304
  731.2 34.2 %copy-start.3 = (f32[8,128,768]{2,1,0:T(8,128)}, f32[8,128,768]{2,1,0:T(8,128)S(1)}, u32[]{:S(2)}) copy-start(f32[8,128,768]{2,1,0:T(8,128)S(1)} %all-to-all-done.2) | copy-start | bytes 9437188
Sparse Core Ops, SparseCore 0:
  11.0 5.4 sort.21.cloned.1.call-done
  19.7 6.9 sort.23.cloned.1.call-done
  78.0 44.2 reduce-scatter.10
  158.1 52.9 reduce-scatter.8
  596.6 114.0 all-gather.11
  712.3 52.9 all-gather.9
  (2 shorter events, 0.0 us)
